TPU v7x, 512 devices: a whole 4x4x16 slice. The times are simulated.
512 devices in a mesh: rows: 128 (over y, z, core), grp: 4 (over x).
Axes of the slice: x: 4, y: 4, z: 16, core: 2. Of those that a mesh axis runs over, the one named last changes fastest.
Arguments:
- basis: float32 [32, 1048576], P(None, ('rows', 'grp')), may hold values from -0.0078125 to 0.0078125, as said below
- core: float32 [32, 32], replicated, may hold values from -0.3 to 4
- snapshots: bfloat16 [4, 32, 1048576], P(None, 'grp', 'rows'), may hold values from -16 to 16
Outputs:
- new_basis: float32 [32, 1048576], P(None, ('rows', 'grp'))
- new_core: float32 [32, 32], replicated
- first_coeffs: float32 [4, 32, 32], replicated
Inputs may be any that keep to these rules, and one draw needn't show every extreme that they name: `basis`: rows orthonormal up to float32 rounding.
All inputs are finite; a program needn't handle non-finite values.
Results may differ from a plain program's by a relative error of at most 0.0003.
Values may be sent and summed in bfloat16 or wider, within the bound.
No kernel may reach another device: no remote copies, remote signals or barrier semaphores. Data moves between devices by JAX's collectives and lax.ppermute only.
A program may use at most 64 MiB of HBM per device.

v0:
```python
import jax
import jax.numpy as jnp
from jax import lax
from jax.sharding import Mesh
from jax.sharding import PartitionSpec as P

BATCHES = 4
ROWS_GRP = ("rows_0", "rows_1", "rows_2", "grp")
ROWS = ("rows_0", "rows_1", "rows_2")


epsilon = 1e-06


def sent_to_all(shard, axis):
    copies = jnp.broadcast_to(shard, (lax.axis_size(axis), *shard.shape))
    return lax.all_to_all(copies, axis, split_axis=0, concat_axis=0, tiled=True)


def of_everyone(shard, axis):
    return sent_to_all(shard, axis).sum(axis=0)


def one_axis_at_a_time(shard, axes):
    far, near = axes
    nearer = of_everyone(shard, near)
    return of_everyone(nearer, far)


def packed_total(arrays, axis):
    ends = [0]
    for a in arrays:
        ends.append(ends[-1] + a.size)
    so_far = one_axis_at_a_time(jnp.concatenate([a.ravel() for a in arrays]), axis)
    return tuple((so_far[b:e].reshape(a.shape) for a, b, e in zip(arrays, ends, ends[1:])))


def contract_rows(left, right):
    return lax.dot_general(
        left,
        right,
        (((1,), (1,)), ((), ())),
        precision=lax.Precision.HIGHEST,
        preferred_element_type=jnp.float32,
    )


def matmul(left, right):
    return jnp.dot(left, right, precision=lax.Precision.HIGHEST, preferred_element_type=jnp.float32)


def lower_solve(factor, right):
    return lax.linalg.triangular_solve(factor, right, left_side=True, lower=True)


def small_update(core_now, total, lower):
    rank = core_now.shape[0]
    cols = lower.shape[0]
    top = jnp.concatenate([core_now, total], axis=1)
    bottom = jnp.concatenate([jnp.zeros((cols, rank), jnp.float32), lower.T], axis=1)
    stacked = jnp.concatenate([top, bottom], axis=0)
    moment = matmul(stacked, stacked.T)
    leading = moment[:, :rank]
    factor = jnp.linalg.cholesky(matmul(leading.T, leading))
    rotation = lower_solve(factor, leading.T).T
    fresh_core = jnp.linalg.cholesky(matmul(rotation.T, matmul(moment, rotation)))
    return (rotation, fresh_core)


def body(basis, core, snapshots):
    rank = basis.shape[0]
    basis_now = basis
    core_now = core
    firsts = []
    gram_basis = one_axis_at_a_time(
        contract_rows(basis_now, basis_now), (("rows_0", "rows_1"), ("rows_2", "grp"))
    )
    for batch in range(BATCHES):
        columns = lax.all_to_all(snapshots[batch], "grp", split_axis=1, concat_axis=0, tiled=True)
        raw = columns.astype(jnp.float32)
        raw_cross, raw_gram = packed_total(
            (contract_rows(basis_now, raw), contract_rows(raw, raw)),
            (("rows_0", "rows_1"), ("rows_2", "grp")),
        )
        inverse = lax.rsqrt(jnp.diagonal(raw_gram) + epsilon)
        scaled = raw * inverse[:, None]
        cross = raw_cross * inverse[None, :]
        gram_raw = raw_gram * inverse[:, None] * inverse[None, :]
        second = cross - matmul(gram_basis, cross)
        total = cross + second
        basis_cross = cross - matmul(gram_basis, total)
        gram = (
            gram_raw
            - matmul(total.T, cross)
            - matmul(cross.T, total)
            + matmul(total.T, matmul(gram_basis, total))
        )
        twice = scaled - matmul(total.T, basis_now)
        lower = jnp.linalg.cholesky(gram)
        fresh = lower_solve(lower, twice)
        rotation, core_now = small_update(core_now, total, lower)
        cross_fresh = lower_solve(lower, basis_cross.T).T
        halfway = lower_solve(lower, gram)
        gram_fresh = lower_solve(lower, halfway.T).T
        upper_block = jnp.concatenate([gram_basis, cross_fresh], axis=1)
        lower_block = jnp.concatenate([cross_fresh.T, gram_fresh], axis=1)
        combined = jnp.concatenate([upper_block, lower_block], axis=0)
        gram_basis = matmul(rotation.T, matmul(combined, rotation))
        firsts.append(cross)
        basis_now = matmul(rotation[:rank].T, basis_now) + matmul(rotation[rank:].T, fresh)
    return (basis_now, core_now, jnp.stack(firsts, axis=0))


def solution(mesh):
    finer = Mesh(
        mesh.devices.reshape(4, 16, 2, mesh.shape["grp"]), ("rows_0", "rows_1", "rows_2", "grp")
    )
    return jax.shard_map(
        body,
        mesh=finer,
        in_specs=(P(None, ROWS_GRP), P(), P(None, "grp", ROWS)),
        out_specs=(P(None, ROWS_GRP), P(), P()),
        check_vma=False,
    )
```

profile of v0, /device:TPU:1, one launch (start us, length us, event | category | flops | bytes accessed | tf_op | source)
XLA Modules:
  0.0 359.8 jit_solution(13954149808816243832)
XLA Ops:
  2.6 4.8 %all-to-all-start = ((bf16[8,4,2048]{2,0,1:T(8,128)(2,1)}), bf16[8,4,2048]{2,0,1:T(8,128)(2,1)S(1)}, u32[]{:S(2)}, u32[]{:S(2)}) async-start(bf16[8,4,2048]{2,0,1:T(8,128)(2,1)} %bitcast), calls=%async_computation | async-start | bytes 262144 | tf_op jit(solution)/shard_map/all_to_all | solution.py:79
  8.5 3.7 %all-to-all-done = bf16[8,4,2048]{2,0,1:T(8,128)(2,1)S(1)} async-done(((bf16[8,4,2048]{2,0,1:T(8,128)(2,1)}), bf16[8,4,2048]{2,0,1:T(8,128)(2,1)S(1)}, u32[]{:S(2)}, u32[]{:S(2)}) %all-to-all-start) | async-done | bytes 131104 | tf_op jit(solution)/shard_map/all_to_all | solution.py:79
  12.2 9.7 %all-to-all-start.3 = ((f32[8,1,1024]{2,1,0:T(1,128)}), f32[8,1,1024]{2,1,0:T(1,128)S(1)}, u32[]{:S(2)}, u32[]{:S(2)}) async-start(f32[8,1,1024]{2,1,0:T(1,128)} %reshape.487), calls=%async_computation.3 | async-start | bytes 65536 | tf_op jit(solution)/shard_map/all_to_all | solution.py:17
  22.2 4.7 %all-to-all-done.3 = f32[8,1,1024]{2,1,0:T(1,128)S(1)} async-done(((f32[8,1,1024]{2,1,0:T(1,128)}), f32[8,1,1024]{2,1,0:T(1,128)S(1)}, u32[]{:S(2)}, u32[]{:S(2)}) %all-to-all-start.3) | async-done | bytes 32800 | tf_op jit(solution)/shard_map/all_to_all | solution.py:17
  26.9 3.3 all-to-all-start.5
  30.5 4.5 %all-to-all-done.5 = bf16[8,4,2048]{2,0,1:T(8,128)(2,1)S(1)} async-done(((bf16[8,4,2048]{2,0,1:T(8,128)(2,1)}), bf16[8,4,2048]{2,0,1:T(8,128)(2,1)S(1)}, u32[]{:S(2)}, u32[]{:S(2)}) %all-to-all-start.5) | async-done | bytes 131104 | tf_op jit(solution)/shard_map/all_to_all | solution.py:79
  35.0 3.3 all-to-all-start.8
  38.3 4.8 %all-to-all-done.8 = bf16[8,4,2048]{2,0,1:T(8,128)(2,1)S(1)} async-done(((bf16[8,4,2048]{2,0,1:T(8,128)(2,1)}), bf16[8,4,2048]{2,0,1:T(8,128)(2,1)S(1)}, u32[]{:S(2)}, u32[]{:S(2)}) %all-to-all-start.8) | async-done | bytes 131104 | tf_op jit(solution)/shard_map/all_to_all | solution.py:79
  43.8 6.0 %all-to-all-start.1 = ((f32[8,1,2048]{2,1,0:T(1,128)}), f32[8,1,2048]{2,1,0:T(1,128)S(1)}, u32[]{:S(2)}, u32[]{:S(2)}) async-start(f32[8,1,2048]{2,1,0:T(1,128)} %broadcast_in_dim.31), calls=%async_computation.1 | async-start | bytes 131072 | tf_op jit(solution)/shard_map/all_to_all | solution.py:17
  54.7 14.1 %all-to-all-start.4 = ((f32[64,1,1024]{2,1,0:T(1,128)}), f32[64,1,1024]{2,1,0:T(1,128)S(1)}, u32[]{:S(2)}, u32[]{:S(2)}) async-start(f32[64,1,1024]{2,1,0:T(1,128)} %reshape.489), calls=%async_computation.4 | async-start | bytes 524288 | tf_op jit(solution)/shard_map/all_to_all | solution.py:17
  68.9 19.8 %all-to-all-done.4 = f32[64,1,1024]{2,1,0:T(1,128)S(1)} async-done(((f32[64,1,1024]{2,1,0:T(1,128)}), f32[64,1,1024]{2,1,0:T(1,128)S(1)}, u32[]{:S(2)}, u32[]{:S(2)}) %all-to-all-start.4) | async-done | bytes 262176 | tf_op jit(solution)/shard_map/all_to_all | solution.py:17
  89.7 7.1 %all-to-all-start.2 = ((f32[64,1,2048]{2,1,0:T(1,128)}), f32[64,1,2048]{2,1,0:T(1,128)S(1)}, u32[]{:S(2)}, u32[]{:S(2)}) async-start(f32[64,1,2048]{2,1,0:T(1,128)} %broadcast_in_dim.58), calls=%async_computation.2 | async-start | bytes 1048576 | tf_op jit(solution)/shard_map/all_to_all | solution.py:17
  99.0 27.0 %all-to-all-done.2 = f32[64,1,2048]{2,1,0:T(1,128)S(1)} async-done(((f32[64,1,2048]{2,1,0:T(1,128)}), f32[64,1,2048]{2,1,0:T(1,128)S(1)}, u32[]{:S(2)}, u32[]{:S(2)}) %all-to-all-start.2) | async-done | bytes 524320 | tf_op jit(solution)/shard_map/all_to_all | solution.py:17
  126.0 3.3 all-to-all-start.11
  136.6 2.9 cholesky.205
  148.6 7.9 %all-to-all-start.6 = ((f32[8,1,2048]{2,1,0:T(1,128)}), f32[8,1,2048]{2,1,0:T(1,128)S(1)}, u32[]{:S(2)}, u32[]{:S(2)}) async-start(f32[8,1,2048]{2,1,0:T(1,128)} %broadcast_in_dim.61), calls=%async_computation.6 | async-start | bytes 131072 | tf_op jit(solution)/shard_map/all_to_all | solution.py:17
  156.9 4.6 %all-to-all-done.6 = f32[8,1,2048]{2,1,0:T(1,128)S(1)} async-done(((f32[8,1,2048]{2,1,0:T(1,128)}), f32[8,1,2048]{2,1,0:T(1,128)S(1)}, u32[]{:S(2)}, u32[]{:S(2)}) %all-to-all-start.6) | async-done | bytes 65568 | tf_op jit(solution)/shard_map/all_to_all | solution.py:17
  162.6 6.9 %all-to-all-start.7 = ((f32[64,1,2048]{2,1,0:T(1,128)}), f32[64,1,2048]{2,1,0:T(1,128)S(1)}, u32[]{:S(2)}, u32[]{:S(2)}) async-start(f32[64,1,2048]{2,1,0:T(1,128)} %broadcast_in_dim.62), calls=%async_computation.7 | async-start | bytes 1048576 | tf_op jit(solution)/shard_map/all_to_all | solution.py:17
  170.3 2.9 cholesky.216
  175.5 23.5 %all-to-all-done.7 = f32[64,1,2048]{2,1,0:T(1,128)S(1)} async-done(((f32[64,1,2048]{2,1,0:T(1,128)}), f32[64,1,2048]{2,1,0:T(1,128)S(1)}, u32[]{:S(2)}, u32[]{:S(2)}) %all-to-all-start.7) | async-done | bytes 524320 | tf_op jit(solution)/shard_map/all_to_all | solution.py:17
  206.3 2.9 cholesky.238
  218.3 6.5 %all-to-all-start.9 = ((f32[8,1,2048]{2,1,0:T(1,128)}), f32[8,1,2048]{2,1,0:T(1,128)S(1)}, u32[]{:S(2)}, u32[]{:S(2)}) async-start(f32[8,1,2048]{2,1,0:T(1,128)} %broadcast_in_dim.63), calls=%async_computation.9 | async-start | bytes 131072 | tf_op jit(solution)/shard_map/all_to_all | solution.py:17
  224.8 4.9 %all-to-all-done.9 = f32[8,1,2048]{2,1,0:T(1,128)S(1)} async-done(((f32[8,1,2048]{2,1,0:T(1,128)}), f32[8,1,2048]{2,1,0:T(1,128)S(1)}, u32[]{:S(2)}, u32[]{:S(2)}) %all-to-all-start.9) | async-done | bytes 65568 | tf_op jit(solution)/shard_map/all_to_all | solution.py:17
  230.8 6.4 %all-to-all-start.10 = ((f32[64,1,2048]{2,1,0:T(1,128)}), f32[64,1,2048]{2,1,0:T(1,128)S(1)}, u32[]{:S(2)}, u32[]{:S(2)}) async-start(f32[64,1,2048]{2,1,0:T(1,128)} %broadcast_in_dim.64), calls=%async_computation.10 | async-start | bytes 1048576 | tf_op jit(solution)/shard_map/all_to_all | solution.py:17
  238.0 2.9 cholesky.249
  243.2 23.8 %all-to-all-done.10 = f32[64,1,2048]{2,1,0:T(1,128)S(1)} async-done(((f32[64,1,2048]{2,1,0:T(1,128)}), f32[64,1,2048]{2,1,0:T(1,128)S(1)}, u32[]{:S(2)}, u32[]{:S(2)}) %all-to-all-start.10) | async-done | bytes 524320 | tf_op jit(solution)/shard_map/all_to_all | solution.py:17
  274.3 2.9 cholesky.271
  286.2 6.4 %all-to-all-start.12 = ((f32[8,1,2048]{2,1,0:T(1,128)}), f32[8,1,2048]{2,1,0:T(1,128)S(1)}, u32[]{:S(2)}, u32[]{:S(2)}) async-start(f32[8,1,2048]{2,1,0:T(1,128)} %broadcast_in_dim.65), calls=%async_computation.12 | async-start | bytes 131072 | tf_op jit(solution)/shard_map/all_to_all | solution.py:17
  292.9 4.7 %all-to-all-done.12 = f32[8,1,2048]{2,1,0:T(1,128)S(1)} async-done(((f32[8,1,2048]{2,1,0:T(1,128)}), f32[8,1,2048]{2,1,0:T(1,128)S(1)}, u32[]{:S(2)}, u32[]{:S(2)}) %all-to-all-start.12) | async-done | bytes 65568 | tf_op jit(solution)/shard_map/all_to_all | solution.py:17
  298.7 6.6 %all-to-all-start.13 = ((f32[64,1,2048]{2,1,0:T(1,128)}), f32[64,1,2048]{2,1,0:T(1,128)S(1)}, u32[]{:S(2)}, u32[]{:S(2)}) async-start(f32[64,1,2048]{2,1,0:T(1,128)} %broadcast_in_dim.66), calls=%async_computation.13 | async-start | bytes 1048576 | tf_op jit(solution)/shard_map/all_to_all | solution.py:17
  305.9 2.9 cholesky.282
  311.1 23.8 %all-to-all-done.13 = f32[64,1,2048]{2,1,0:T(1,128)S(1)} async-done(((f32[64,1,2048]{2,1,0:T(1,128)}), f32[64,1,2048]{2,1,0:T(1,128)S(1)}, u32[]{:S(2)}, u32[]{:S(2)}) %all-to-all-start.13) | async-done | bytes 524320 | tf_op jit(solution)/shard_map/all_to_all | solution.py:17
  (247 shorter events, 98.7 us)
Async XLA Ops:
  0.6 6.8 %copy-start = (f32[32,2048]{1,0:T(8,128)S(1)}, f32[32,2048]{1,0:T(8,128)}, u32[]{:S(2)}) copy-start(f32[32,2048]{1,0:T(8,128)} %param.10) | copy-start | bytes 786436
  2.6 9.7 %all-to-all-start = ((bf16[8,4,2048]{2,0,1:T(8,128)(2,1)}), bf16[8,4,2048]{2,0,1:T(8,128)(2,1)S(1)}, u32[]{:S(2)}, u32[]{:S(2)}) async-start(bf16[8,4,2048]{2,0,1:T(8,128)(2,1)} %bitcast), calls=%async_computation | async-start | bytes 262144 | tf_op jit(solution)/shard_map/all_to_all | solution.py:79
  12.2 14.6 %all-to-all-start.3 = ((f32[8,1,1024]{2,1,0:T(1,128)}), f32[8,1,1024]{2,1,0:T(1,128)S(1)}, u32[]{:S(2)}, u32[]{:S(2)}) async-start(f32[8,1,1024]{2,1,0:T(1,128)} %reshape.487), calls=%async_computation.3 | async-start | bytes 65536 | tf_op jit(solution)/shard_map/all_to_all | solution.py:17
  26.9 8.1 %all-to-all-start.5 = ((bf16[8,4,2048]{2,0,1:T(8,128)(2,1)}), bf16[8,4,2048]{2,0,1:T(8,128)(2,1)S(1)}, u32[]{:S(2)}, u32[]{:S(2)}) async-start(bf16[8,4,2048]{2,0,1:T(8,128)(2,1)} %bitcast.15), calls=%async_computation.5 | async-start | bytes 262144 | tf_op jit(solution)/shard_map/all_to_all | solution.py:79
  35.0 8.1 %all-to-all-start.8 = ((bf16[8,4,2048]{2,0,1:T(8,128)(2,1)}), bf16[8,4,2048]{2,0,1:T(8,128)(2,1)S(1)}, u32[]{:S(2)}, u32[]{:S(2)}) async-start(bf16[8,4,2048]{2,0,1:T(8,128)(2,1)} %bitcast.39), calls=%async_computation.8 | async-start | bytes 262144 | tf_op jit(solution)/shard_map/all_to_all | solution.py:79
  43.8 10.9 %all-to-all-start.1 = ((f32[8,1,2048]{2,1,0:T(1,128)}), f32[8,1,2048]{2,1,0:T(1,128)S(1)}, u32[]{:S(2)}, u32[]{:S(2)}) async-start(f32[8,1,2048]{2,1,0:T(1,128)} %broadcast_in_dim.31), calls=%async_computation.1 | async-start | bytes 131072 | tf_op jit(solution)/shard_map/all_to_all | solution.py:17
  54.7 33.9 %all-to-all-start.4 = ((f32[64,1,1024]{2,1,0:T(1,128)}), f32[64,1,1024]{2,1,0:T(1,128)S(1)}, u32[]{:S(2)}, u32[]{:S(2)}) async-start(f32[64,1,1024]{2,1,0:T(1,128)} %reshape.489), calls=%async_computation.4 | async-start | bytes 524288 | tf_op jit(solution)/shard_map/all_to_all | solution.py:17
  89.7 7.1 %copy-start.1 = (f32[32,32]{1,0:T(8,128)S(1)}, f32[32,32]{1,0:T(8,128)}, u32[]{:S(2)}) copy-start(f32[32,32]{1,0:T(8,128)} %param.11) | copy-start | bytes 12292
  89.7 36.3 %all-to-all-start.2 = ((f32[64,1,2048]{2,1,0:T(1,128)}), f32[64,1,2048]{2,1,0:T(1,128)S(1)}, u32[]{:S(2)}, u32[]{:S(2)}) async-start(f32[64,1,2048]{2,1,0:T(1,128)} %broadcast_in_dim.58), calls=%async_computation.2 | async-start | bytes 1048576 | tf_op jit(solution)/shard_map/all_to_all | solution.py:17
  126.0 21.9 %all-to-all-start.11 = ((bf16[8,4,2048]{2,0,1:T(8,128)(2,1)}), bf16[8,4,2048]{2,0,1:T(8,128)(2,1)S(1)}, u32[]{:S(2)}, u32[]{:S(2)}) async-start(bf16[8,4,2048]{2,0,1:T(8,128)(2,1)} %bitcast.63), calls=%async_computation.11 | async-start | bytes 262144 | tf_op jit(solution)/shard_map/all_to_all | solution.py:79
  148.6 12.9 %all-to-all-start.6 = ((f32[8,1,2048]{2,1,0:T(1,128)}), f32[8,1,2048]{2,1,0:T(1,128)S(1)}, u32[]{:S(2)}, u32[]{:S(2)}) async-start(f32[8,1,2048]{2,1,0:T(1,128)} %broadcast_in_dim.61), calls=%async_computation.6 | async-start | bytes 131072 | tf_op jit(solution)/shard_map/all_to_all | solution.py:17
  162.6 36.4 %all-to-all-start.7 = ((f32[64,1,2048]{2,1,0:T(1,128)}), f32[64,1,2048]{2,1,0:T(1,128)S(1)}, u32[]{:S(2)}, u32[]{:S(2)}) async-start(f32[64,1,2048]{2,1,0:T(1,128)} %broadcast_in_dim.62), calls=%async_computation.7 | async-start | bytes 1048576 | tf_op jit(solution)/shard_map/all_to_all | solution.py:17
  218.3 11.4 %all-to-all-start.9 = ((f32[8,1,2048]{2,1,0:T(1,128)}), f32[8,1,2048]{2,1,0:T(1,128)S(1)}, u32[]{:S(2)}, u32[]{:S(2)}) async-start(f32[8,1,2048]{2,1,0:T(1,128)} %broadcast_in_dim.63), calls=%async_computation.9 | async-start | bytes 131072 | tf_op jit(solution)/shard_map/all_to_all | solution.py:17
  230.8 36.1 %all-to-all-start.10 = ((f32[64,1,2048]{2,1,0:T(1,128)}), f32[64,1,2048]{2,1,0:T(1,128)S(1)}, u32[]{:S(2)}, u32[]{:S(2)}) async-start(f32[64,1,2048]{2,1,0:T(1,128)} %broadcast_in_dim.64), calls=%async_computation.10 | async-start | bytes 1048576 | tf_op jit(solution)/shard_map/all_to_all | solution.py:17
  286.2 11.4 %all-to-all-start.12 = ((f32[8,1,2048]{2,1,0:T(1,128)}), f32[8,1,2048]{2,1,0:T(1,128)S(1)}, u32[]{:S(2)}, u32[]{:S(2)}) async-start(f32[8,1,2048]{2,1,0:T(1,128)} %broadcast_in_dim.65), calls=%async_computation.12 | async-start | bytes 131072 | tf_op jit(solution)/shard_map/all_to_all | solution.py:17
  298.7 36.1 %all-to-all-start.13 = ((f32[64,1,2048]{2,1,0:T(1,128)}), f32[64,1,2048]{2,1,0:T(1,128)S(1)}, u32[]{:S(2)}, u32[]{:S(2)}) async-start(f32[64,1,2048]{2,1,0:T(1,128)} %broadcast_in_dim.66), calls=%async_computation.13 | async-start | bytes 1048576 | tf_op jit(solution)/shard_map/all_to_all | solution.py:17
where the time goes:
time: 363 us; the launch traced here: 360 us
  waiting for transfers between devices  152 us (42%)
  starting transfers between devices  92.4 us (25%)
  other arithmetic  75.8 us (21%)
  matrix products  19.8 us (5%)
  local copies, waits for them, and re-layouts  18.3 us (5%)
    all_to_all x10, waiting for transfers between devices, sent_to_all(): return lax.all_to_all(copies, axis, split_axis=0, concat_axis=0, tiled=True)  139 us
    all_to_all x10, starting transfers between devices, sent_to_all(): return lax.all_to_all(copies, axis, split_axis=0, concat_axis=0, tiled=True)  77.6 us
    another operation x16, other arithmetic, lower_solve(): lax.linalg.triangular_solve(factor, right, left_side=True, lower=True)  24.7 us
    all_to_all x4, starting transfers between devices, body(): lax.all_to_all(snapshots[batch], 'grp', split_axis=1, concat_axis=0, tile...  14.8 us
    another operation x12, other arithmetic, small_update(): jnp.linalg.cholesky(matmul(rotation.T, matmul(moment, rotation)))  14.7 us
    another operation x12, other arithmetic, small_update(): factor = jnp.linalg.cholesky(matmul(leading.T, leading))  14.4 us
    another operation x12, other arithmetic, body(): lower = jnp.linalg.cholesky(gram)  14.4 us
    dot_general x54, matrix products, matmul(): jnp.dot(left, right, precision=lax.Precision.HIGHEST, preferred_element_t...  13.5 us
  transfers between devices with their start and end apart: 14, of which 13 were waited for; matrix products, arithmetic and copies ran while one was open for 12% of the time, Pallas kernels for 0%

commit v1 on v0

v1 whole, which is shorter than its diff:
```python
import jax
import jax.numpy as jnp
from jax import lax
from jax.experimental import pallas as pl
from jax.experimental.pallas import tpu as pltpu
from jax.sharding import Mesh
from jax.sharding import PartitionSpec as P

BATCHES = 4
ROWS_GRP = ("rows_0", "rows_1", "rows_2", "grp")
ROWS = ("rows_0", "rows_1", "rows_2")
NEAR = ("rows_0", "rows_2", "grp")
FAR = "rows_1"
LANES = 128
SUB = 8

epsilon = 1e-06


def exchange(parts, axis):
    return lax.all_to_all(parts, axis, split_axis=0, concat_axis=0, tiled=True)


def total_over_all(packed):
    near = lax.axis_size(NEAR)
    far = lax.axis_size(FAR)
    rows, lanes = packed.shape
    piece = exchange(packed.reshape(near, rows // near, lanes), NEAR).sum(axis=0)
    piece = exchange(jnp.broadcast_to(piece, (far, *piece.shape)), FAR).sum(axis=0)
    return exchange(jnp.broadcast_to(piece, (near, *piece.shape)), NEAR).reshape(rows, lanes)


def dot(left, right, contract=(1, 0)):
    return lax.dot_general(
        left,
        right,
        (((contract[0],), (contract[1],)), ((), ())),
        precision=lax.Precision.HIGHEST,
        preferred_element_type=jnp.float32,
    )


def dot_short(left, right, contract=(1, 0)):
    return lax.dot_general(
        left,
        right,
        (((contract[0],), (contract[1],)), ((), ())),
        preferred_element_type=jnp.float32,
    )


def three_parts(values):
    high = values.astype(jnp.bfloat16)
    rest = values - high.astype(jnp.float32)
    middle = rest.astype(jnp.bfloat16)
    low = (rest - middle.astype(jnp.float32)).astype(jnp.bfloat16)
    return high, middle, low


def by_batch(received):
    groups, batches, cols, dofs = received.shape
    return [
        jnp.concatenate([received[g, b] for g in range(groups)], axis=0) for b in range(batches)
    ]


def gram_kernel(received_ref, basis_ref, packed_ref):
    raw = jnp.concatenate(by_batch(received_ref[...]), axis=0)
    parts = jnp.concatenate(three_parts(basis_ref[...]), axis=0)
    cols = raw.shape[0]
    rank = basis_ref.shape[0]
    raw_gram = dot_short(raw, raw, (1, 1))
    cross = dot_short(parts, raw, (1, 1))
    square = dot_short(parts, parts, (1, 1))
    cross = cross[2 * rank :] + cross[rank : 2 * rank] + cross[:rank]
    square = square[2 * rank :] + square[rank : 2 * rank] + square[:rank]
    square = square[:, 2 * rank :] + square[:, rank : 2 * rank] + square[:, :rank]
    step = cols // BATCHES
    packed_ref[0:step] = raw_gram[0:step]
    packed_ref[step : 2 * step] = jnp.concatenate(
        [raw_gram[3 * step :, 3 * step :], raw_gram[step : 2 * step, step:]], axis=1
    )
    packed_ref[2 * step : 3 * step] = jnp.concatenate(
        [square, raw_gram[2 * step : 3 * step, step:]], axis=1
    )
    packed_ref[3 * step :] = cross


def eliminate(matrix, want_inverse):
    order = matrix.shape[0]
    tiles = order // SUB
    work = [matrix[SUB * g : SUB * g + SUB] for g in range(tiles)]
    row = lax.broadcasted_iota(jnp.int32, (SUB, order), 0)
    lane = lax.broadcasted_iota(jnp.int32, (SUB, order), 1)
    inverse = [jnp.where(row + SUB * g == lane, 1.0, 0.0) for g in range(tiles)]
    lower = [jnp.zeros((SUB, order), jnp.float32) for g in range(tiles)]

    def spread(tile, k):
        return jnp.broadcast_to(tile[k : k + 1], (SUB, order))

    for p in range(tiles):
        columns = {
            (m, g): jnp.broadcast_to(work[g][:, SUB * p + m : SUB * p + m + 1], (SUB, order))
            for m in range(SUB)
            for g in range(p, tiles)
        }
        scale = jnp.zeros((SUB, order), jnp.float32)
        for k in range(SUB):
            pivot = spread(columns[k, p], k)
            root = lax.rsqrt(pivot)
            recip = 1.0 / pivot
            scale = jnp.where(row == k, root, scale)
            factors = {g: columns[k, g] * recip for g in range(p, tiles)}
            factors[p] = jnp.where(row > k, factors[p], 0.0)
            if not want_inverse:
                for g in range(p, tiles):
                    part = columns[k, g] * root
                    if g == p:
                        part = jnp.where(row >= k, part, 0.0)
                    lower[g] = jnp.where(lane == SUB * p + k, part, lower[g])
            for m in range(k + 1, SUB):
                top = spread(columns[m, p], k)
                for g in range(p, tiles):
                    columns[m, g] = columns[m, g] - factors[g] * top
            top = spread(work[p], k)
            for g in range(p + 1, tiles):
                work[g] = work[g] - factors[g] * top
            work[p] = work[p] - factors[p] * top
            if want_inverse:
                top = spread(inverse[p], k)
                for g in range(p, tiles):
                    inverse[g] = inverse[g] - factors[g] * top
        if want_inverse:
            inverse[p] = inverse[p] * scale
    return jnp.concatenate(inverse if want_inverse else lower, axis=0)


def unpacked(packed, cols):
    step = cols // BATCHES
    rank = packed.shape[0] - 3 * step
    row = lax.broadcasted_iota(jnp.int32, packed.shape, 0)
    lane = lax.broadcasted_iota(jnp.int32, packed.shape, 1)
    own = jnp.where(row == lane, packed, 0.0)[: 3 * step]
    last = jnp.where(row - step == lane, packed, 0.0)[step : 2 * step, :step]
    across = jnp.concatenate(
        [jnp.sum(own, axis=0, keepdims=True)[:, : 3 * step], jnp.sum(last, axis=0, keepdims=True)],
        axis=1,
    )
    across = lax.rsqrt(across + epsilon)
    down = [jnp.sum(own[step * b : step * b + step], axis=1, keepdims=True) for b in range(3)]
    down = [lax.rsqrt(d + epsilon) for d in down + [jnp.sum(last, axis=1, keepdims=True)]]
    rows = [packed[step * b : step * b + step] * across * down[b] for b in range(3)]
    grams = [rows[b][:, step * b : step * b + step] for b in range(3)]
    grams.append(packed[step : 2 * step, :step] * across[:, 3 * step :] * down[3])
    cross = packed[3 * step :] * across
    return cross, packed[2 * step : 3 * step, :rank], rows, grams, across


def update_kernel(packed_ref, core_ref, basis_ref, received_ref, new_basis_ref, new_core_ref, firsts_ref):
    received = received_ref[...]
    cols = received.shape[0] * received.shape[1] * received.shape[2]
    step = cols // BATCHES
    cross, gram_basis, rows, grams, across = unpacked(packed_ref[...], cols)
    root = core_ref[...]
    energy = dot(root, root, (1, 1))
    of_basis = None
    of_raw = None
    for b in range(BATCHES):
        first = cross[:, step * b : step * b + step]
        firsts_ref[b] = first
        second = first - dot(gram_basis, first)
        total = first + second
        rest = first - dot(gram_basis, total)
        gram = grams[b] - dot(first, total, (0, 0)) - dot(total, rest, (0, 0))
        leading = energy + dot(total, total, (1, 1))
        total_gram = dot(total, gram)
        square = dot(leading, leading) + dot(total_gram, total, (1, 1))
        tail = dot(leading, total)
        inverse = eliminate(square, True)
        from_old = dot(inverse, energy)
        from_new = dot(inverse, total)
        root = dot(inverse, dot(leading, root))
        tail = dot(inverse, tail) + dot(inverse, total_gram)
        energy = dot(root, root, (1, 1)) + dot(tail, tail, (1, 1))
        if b + 1 < BATCHES:
            root = jnp.concatenate([root, tail], axis=1)
            left = dot(from_old, gram_basis) + dot(from_new, first, (1, 1))
            right = dot(from_old, first) + dot(from_new, grams[b])
            gram_basis = dot(left, from_old, (1, 1)) + dot(right, from_new, (1, 1))
            cross = dot(from_old, cross) + dot(from_new, rows[b])
        if b == 0:
            of_basis = from_old
            of_raw = from_new
        else:
            of_basis = dot(from_old, of_basis)
            of_raw = jnp.concatenate([dot(from_old, of_raw), from_new], axis=1)
    new_core_ref[...] = eliminate(energy, False)
    of_raw = of_raw * across
    raw = jnp.concatenate(by_batch(received), axis=0)
    parts = dot_short(jnp.concatenate(three_parts(of_raw), axis=0), raw)
    rank = of_raw.shape[0]
    new_basis_ref[...] = (
        dot(of_basis, basis_ref[...]) + parts[2 * rank :] + parts[rank : 2 * rank] + parts[:rank]
    )


def body(basis, core, snapshots):
    batches, mine, dofs = snapshots.shape
    grp = lax.axis_size("grp")
    rank = basis.shape[0]
    cols = grp * mine
    pieces = snapshots.reshape(batches, mine, grp, dofs // grp).transpose(2, 0, 1, 3)
    received = exchange(pieces, "grp")
    packed = pl.pallas_call(
        gram_kernel, out_shape=jax.ShapeDtypeStruct((3 * cols + rank, LANES), jnp.float32)
    )(received, basis)
    packed = total_over_all(packed)
    return pl.pallas_call(
        update_kernel,
        out_shape=(
            jax.ShapeDtypeStruct(basis.shape, jnp.float32),
            jax.ShapeDtypeStruct(core.shape, jnp.float32),
            jax.ShapeDtypeStruct((batches, rank, cols), jnp.float32),
        ),
    )(packed, core, basis, received)


def solution(mesh):
    finer = Mesh(
        mesh.devices.reshape(4, 16, 2, mesh.shape["grp"]), ("rows_0", "rows_1", "rows_2", "grp")
    )
    return jax.shard_map(
        body,
        mesh=finer,
        in_specs=(P(None, ROWS_GRP), P(), P(None, "grp", ROWS)),
        out_specs=(P(None, ROWS_GRP), P(), P()),
        check_vma=False,
    )
```

time: 363 us -> 84.2 us (0.23)
  waiting for transfers between devices: 152 us -> 0 us
  starting transfers between devices: 92.4 us -> 0 us
  other arithmetic: 75.8 us -> 0.07 us
  blocking collectives: 0 us -> 66.3 us
  matrix products: 19.8 us -> 0 us
  local copies, waits for them, and re-layouts: 18.3 us -> 1.1 us
  Pallas kernels: 0 us -> 15.7 us
    all_to_all x14 -> x0, waiting for transfers between devices: 152 us -> none  [the longest x10 139 us: sent_to_all(): return lax.all_to_all(copies, axis, split_axis=0, concat_axis=0, tiled=True)]
    all_to_all x14 -> x0, starting transfers between devices: 92.4 us -> none  [the longest x10 77.6 us: sent_to_all(): return lax.all_to_all(copies, axis, split_axis=0, concat_axis=0, tiled=True)]
    another operation x53 -> x0, other arithmetic: 68.8 us -> none  [the longest x16 24.7 us: lower_solve(): lax.linalg.triangular_solve(factor, right, left_side=True, lower=True)]
    all_to_all x0 -> x4, blocking collectives: none -> 66.3 us  [exchange(): return lax.all_to_all(parts, axis, split_axis=0, concat_axis=0, tiled=True)]
    pallas_call x0 -> x2, Pallas kernels: none -> 15.7 us  [the longest x1 13.2 us: body(): pl.pallas_call(update_kernel, out_shape=(jax.ShapeDtypeStruct(basis.shape...]
    dot_general x63 -> x0, matrix products: 15.5 us -> none  [the longest x54 13.5 us: matmul(): jnp.dot(left, right, precision=lax.Precision.HIGHEST, preferred_element_t...]
    broadcast_in_dim x10 -> x2, local copies, waits for them, and re-layouts: 7.03 us -> 0.02 us  [the longest x1 0.01 us: total_over_all(): jnp.broadcast_to(piece, (near, *piece.shape))]
    another operation x17 -> x0, matrix products: 4.33 us -> none  [lower_solve(): lax.linalg.triangular_solve(factor, right, left_side=True, lower=True)]
  transfers between devices with their start and end apart: 14 -> 0, of which waited for: 13 -> 0; matrix products, arithmetic and copies ran while one was open for 12% -> 0% of each run, Pallas kernels for 0% -> 0%
where the time goes in v1:
time: 84.2 us; the launch traced here: 83.8 us
  blocking collectives  66.3 us (79%)
  Pallas kernels  15.7 us (19%)
  local copies, waits for them, and re-layouts  1.1 us (1%)
    all_to_all x4, blocking collectives, exchange(): return lax.all_to_all(parts, axis, split_axis=0, concat_axis=0, tiled=True)  66.3 us
    pallas_call x1, Pallas kernels, body(): pl.pallas_call(update_kernel, out_shape=(jax.ShapeDtypeStruct(basis.shape...  13.2 us
    pallas_call x1, Pallas kernels, body(): pl.pallas_call(gram_kernel, out_shape=jax.ShapeDtypeStruct((3 * cols + ra...  2.42 us

profile of v1, /device:TPU:1, one launch (start us, length us, event | category | flops | bytes accessed | tf_op | source)
XLA Modules:
  0.0 83.8 jit_solution(13787635217269427409)
XLA Ops:
  0.6 1.1 %copy.13 = bf16[4,1,4,8,2048]{4,3,1,0,2:T(8,128)(2,1)S(1)} copy(bf16[4,1,4,8,2048]{4,3,2,1,0:T(8,128)(2,1)} %bitcast.10) | data formatting | bytes 1048576 | tf_op jit(solution)/shard_map/reshape | solution.py:212
  1.7 11.7 %all_to_all.20.received_ref = bf16[4,4,8,2048]{3,2,1,0:T(8,128)(2,1)} all-to-all(bf16[4,4,8,2048]{3,2,1,0:T(8,128)(2,1)S(1)} %bitcast.9), channel_id=1, replica_groups=mesh['rows_0'=4,'rows_1'=16,'rows_2'=2,'grp'=4] {'grp'}, dimensions={0} | all-to-all | bytes 1048576 | tf_op jit(solution)/shard_map/all_to_all | solution.py:21
  13.4 2.4 %shard_map.58 = f32[128,128]{1,0:T(8,128)} custom-call(bf16[4,4,8,2048]{3,2,1,0:T(8,128)(2,1)} %all_to_all.20.received_ref, f32[32,2048]{1,0:T(8,128)} %basis_ref.3), custom_call_target="tpu_custom_call" | custom-call | tf_op jit(solution)/shard_map/pallas_call | solution.py:214
  15.8 17.2 %all_to_all.21 = f32[32,4,128]{2,1,0:T(4,128)S(1)} all-to-all(f32[32,4,128]{2,1,0:T(4,128)} %bitcast.12), channel_id=1, replica_groups=mesh['rows_0'=4,'rows_1'=16,'rows_2'=2,'grp'=4] {'rows_0','rows_2','grp'}, dimensions={0} | all-to-all | bytes 131072 | tf_op jit(solution)/shard_map/all_to_all | solution.py:21
  33.1 25.0 %all_to_all.22 = f32[16,4,128]{2,1,0:T(4,128)S(1)} all-to-all(f32[16,4,128]{2,1,0:T(4,128)S(1)} %broadcast_in_dim.6), channel_id=1, replica_groups=mesh['rows_0'=4,'rows_1'=16,'rows_2'=2,'grp'=4] {'rows_1'}, dimensions={0} | all-to-all | bytes 65536 | tf_op jit(solution)/shard_map/all_to_all | solution.py:21
  58.1 12.5 %all_to_all.23 = f32[32,4,128]{2,1,0:T(4,128)} all-to-all(f32[32,4,128]{2,1,0:T(4,128)S(1)} %broadcast_in_dim.7), channel_id=1, replica_groups=mesh['rows_0'=4,'rows_1'=16,'rows_2'=2,'grp'=4] {'rows_0','rows_2','grp'}, dimensions={0} | all-to-all | bytes 131072 | tf_op jit(solution)/shard_map/all_to_all | solution.py:21
  70.5 13.2 %shard_map.59 = (f32[32,2048]{1,0:T(8,128)}, f32[32,32]{1,0:T(8,128)}, f32[4,32,32]{2,1,0:T(8,128)}) custom-call(f32[128,128]{1,0:T(8,128)} %bitcast.11, f32[32,32]{1,0:T(8,128)} %core_ref.1, f32[32,2048]{1,0:T(8,128)} %basis_ref.3, bf16[4,4,8,2048]{3,2,1,0:T(8,128)(2,1)} %all_to_all.20.received_ref), custom_call_target="tpu_custom_call" | custom-call | tf_op jit(solution)/shard_map/pallas_call | solution.py:218
  (4 shorter events, 0.1 us)

commit v2 on v1

--- a/solution.py
+++ b/solution.py
@@ -13,6 +13,7 @@
 FAR = "rows_1"
 LANES = 128
 SUB = 8
+SMALL_GRANT = pltpu.CompilerParams(vmem_limit_bytes=8 * 2**20)
 
 epsilon = 1e-06
 
@@ -208,11 +209,13 @@
     batches, mine, dofs = snapshots.shape
     grp = lax.axis_size("grp")
     rank = basis.shape[0]
-    cols = grp * mine
+    cols = batches * grp * mine
     pieces = snapshots.reshape(batches, mine, grp, dofs // grp).transpose(2, 0, 1, 3)
     received = exchange(pieces, "grp")
     packed = pl.pallas_call(
-        gram_kernel, out_shape=jax.ShapeDtypeStruct((3 * cols + rank, LANES), jnp.float32)
+        gram_kernel,
+        out_shape=jax.ShapeDtypeStruct((3 * (cols // batches) + rank, LANES), jnp.float32),
+        compiler_params=SMALL_GRANT,
     )(received, basis)
     packed = total_over_all(packed)
     return pl.pallas_call(
@@ -220,8 +223,9 @@
         out_shape=(
             jax.ShapeDtypeStruct(basis.shape, jnp.float32),
             jax.ShapeDtypeStruct(core.shape, jnp.float32),
-            jax.ShapeDtypeStruct((batches, rank, cols), jnp.float32),
+            jax.ShapeDtypeStruct((batches, rank, cols // batches), jnp.float32),
         ),
+        compiler_params=SMALL_GRANT,
     )(packed, core, basis, received)
 
 

time: 84.2 us -> 81 us (0.962)
  Pallas kernels: 15.7 us -> 12.8 us
    pallas_call x1, Pallas kernels: 2.42 us -> 0.67 us  [body(): pl.pallas_call(gram_kernel, out_shape=jax.ShapeDtypeStruct((3 * (cols //...]
    pallas_call x1, Pallas kernels: 13.2 us -> 12.1 us  [body(): pl.pallas_call(update_kernel, out_shape=(jax.ShapeDtypeStruct(basis.shape...]
where the time goes in v2:
time: 81 us; the launch traced here: 80.6 us
  blocking collectives  66 us (81%)
  Pallas kernels  12.8 us (16%)
  local copies, waits for them, and re-layouts  1.11 us (1%)
    all_to_all x4, blocking collectives, exchange(): return lax.all_to_all(parts, axis, split_axis=0, concat_axis=0, tiled=True)  66 us
    pallas_call x1, Pallas kernels, body(): pl.pallas_call(update_kernel, out_shape=(jax.ShapeDtypeStruct(basis.shape...  12.1 us

profile of v2, /device:TPU:1, one launch (start us, length us, event | category | flops | bytes accessed | tf_op | source)
XLA Modules:
  0.0 80.6 jit_solution(5593086219481890292)
XLA Ops:
  0.6 1.1 %copy.13 = bf16[4,1,4,8,2048]{4,3,1,0,2:T(8,128)(2,1)S(1)} copy(bf16[4,1,4,8,2048]{4,3,2,1,0:T(8,128)(2,1)} %bitcast.12) | data formatting | bytes 1048576 | tf_op jit(solution)/shard_map/reshape | solution.py:213
  1.7 0.0 copy-start
  1.7 11.7 %all_to_all.20.received_ref = bf16[4,4,8,2048]{3,2,1,0:T(8,128)(2,1)S(1)} all-to-all(bf16[4,4,8,2048]{3,2,1,0:T(8,128)(2,1)S(1)} %bitcast.11), channel_id=1, replica_groups=mesh['rows_0'=4,'rows_1'=16,'rows_2'=2,'grp'=4] {'grp'}, dimensions={0} | all-to-all | bytes 1048576 | tf_op jit(solution)/shard_map/all_to_all | solution.py:22
  13.4 0.0 copy-done
  13.4 0.7 shard_map.58
  14.1 15.8 %all_to_all.21 = f32[32,4,128]{2,1,0:T(4,128)S(1)} all-to-all(f32[32,4,128]{2,1,0:T(4,128)S(1)} %bitcast.10), channel_id=1, replica_groups=mesh['rows_0'=4,'rows_1'=16,'rows_2'=2,'grp'=4] {'rows_0','rows_2','grp'}, dimensions={0} | all-to-all | bytes 131072 | tf_op jit(solution)/shard_map/all_to_all | solution.py:22
  29.9 26.2 %all_to_all.22 = f32[16,4,128]{2,1,0:T(4,128)S(1)} all-to-all(f32[16,4,128]{2,1,0:T(4,128)S(1)} %broadcast_in_dim.6), channel_id=1, replica_groups=mesh['rows_0'=4,'rows_1'=16,'rows_2'=2,'grp'=4] {'rows_1'}, dimensions={0} | all-to-all | bytes 65536 | tf_op jit(solution)/shard_map/all_to_all | solution.py:22
  56.2 0.0 copy-start.1
  56.2 12.4 %all_to_all.23 = f32[32,4,128]{2,1,0:T(4,128)S(1)} all-to-all(f32[32,4,128]{2,1,0:T(4,128)S(1)} %broadcast_in_dim.7), channel_id=1, replica_groups=mesh['rows_0'=4,'rows_1'=16,'rows_2'=2,'grp'=4] {'rows_0','rows_2','grp'}, dimensions={0} | all-to-all | bytes 131072 | tf_op jit(solution)/shard_map/all_to_all | solution.py:22
  68.5 0.0 copy-done.1
  68.6 12.1 %shard_map.59 = (f32[32,2048]{1,0:T(8,128)}, f32[32,32]{1,0:T(8,128)}, f32[4,32,32]{2,1,0:T(8,128)}) custom-call(f32[128,128]{1,0:T(8,128)S(1)} %bitcast.9, f32[32,32]{1,0:T(8,128)S(1)} %copy-done.1, f32[32,2048]{1,0:T(8,128)S(1)} %copy-done, bf16[4,4,8,2048]{3,2,1,0:T(8,128)(2,1)S(1)} %all_to_all.20.received_ref), custom_call_target="tpu_custom_call" | custom-call | tf_op jit(solution)/shard_map/pallas_call | solution.py:221
  (4 shorter events, 0.1 us)
Async XLA Ops:
  1.7 11.7 %copy-start = (f32[32,2048]{1,0:T(8,128)S(1)}, f32[32,2048]{1,0:T(8,128)}, u32[]{:S(2)}) copy-start(f32[32,2048]{1,0:T(8,128)} %basis_ref.3) | copy-start | bytes 786436
  56.2 12.4 %copy-start.1 = (f32[32,32]{1,0:T(8,128)S(1)}, f32[32,32]{1,0:T(8,128)}, u32[]{:S(2)}) copy-start(f32[32,32]{1,0:T(8,128)} %core_ref.1) | copy-start | bytes 12292

commit v3 on v1

--- a/solution.py
+++ b/solution.py
@@ -13,6 +13,7 @@
 FAR = "rows_1"
 LANES = 128
 SUB = 8
+SMALL_GRANT = pltpu.CompilerParams(vmem_limit_bytes=8 * 2**20)
 
 epsilon = 1e-06
 
@@ -135,94 +136,118 @@
     return jnp.concatenate(inverse if want_inverse else lower, axis=0)
 
 
-def unpacked(packed, cols):
+def update_kernel(
+    packed_ref, core_ref, basis_ref, received_ref, new_basis_ref, new_core_ref, firsts_ref, made_ref, sent
+):
+    cols = packed_ref.shape[1]
     step = cols // BATCHES
-    rank = packed.shape[0] - 3 * step
-    row = lax.broadcasted_iota(jnp.int32, packed.shape, 0)
-    lane = lax.broadcasted_iota(jnp.int32, packed.shape, 1)
-    own = jnp.where(row == lane, packed, 0.0)[: 3 * step]
-    last = jnp.where(row - step == lane, packed, 0.0)[step : 2 * step, :step]
-    across = jnp.concatenate(
-        [jnp.sum(own, axis=0, keepdims=True)[:, : 3 * step], jnp.sum(last, axis=0, keepdims=True)],
-        axis=1,
-    )
-    across = lax.rsqrt(across + epsilon)
-    down = [jnp.sum(own[step * b : step * b + step], axis=1, keepdims=True) for b in range(3)]
-    down = [lax.rsqrt(d + epsilon) for d in down + [jnp.sum(last, axis=1, keepdims=True)]]
-    rows = [packed[step * b : step * b + step] * across * down[b] for b in range(3)]
-    grams = [rows[b][:, step * b : step * b + step] for b in range(3)]
-    grams.append(packed[step : 2 * step, :step] * across[:, 3 * step :] * down[3])
-    cross = packed[3 * step :] * across
-    return cross, packed[2 * step : 3 * step, :rank], rows, grams, across
-
-
-def update_kernel(packed_ref, core_ref, basis_ref, received_ref, new_basis_ref, new_core_ref, firsts_ref):
-    received = received_ref[...]
-    cols = received.shape[0] * received.shape[1] * received.shape[2]
-    step = cols // BATCHES
-    cross, gram_basis, rows, grams, across = unpacked(packed_ref[...], cols)
+    rank = core_ref.shape[0]
+    eye = jnp.where(
+        lax.broadcasted_iota(jnp.int32, (step, step), 0) == lax.broadcasted_iota(jnp.int32, (step, step), 1), 1.0, 0.0
+    )
+    rows = [packed_ref[step * b : step * b + step] for b in range(BATCHES - 1)]
+    cross = packed_ref[3 * step :]
+    grams = [rows[b][:, step * b : step * b + step] for b in range(BATCHES - 1)] + [rows[1][:, :step]]
+    scales = [lax.rsqrt(jnp.sum(g * eye, axis=0, keepdims=True) + epsilon) for g in grams]
+    gram_basis = rows[2][:, :rank]
+    first = cross[:, :step] * scales[0]
     root = core_ref[...]
     energy = dot(root, root, (1, 1))
     of_basis = None
     of_raw = None
     for b in range(BATCHES):
-        first = cross[:, step * b : step * b + step]
+        more = b + 1 < BATCHES
+        scale = scales[b]
         firsts_ref[b] = first
-        second = first - dot(gram_basis, first)
+        defect = eye - gram_basis
+        second = dot(defect, first)
         total = first + second
-        rest = first - dot(gram_basis, total)
-        gram = grams[b] - dot(first, total, (0, 0)) - dot(total, rest, (0, 0))
-        leading = energy + dot(total, total, (1, 1))
-        total_gram = dot(total, gram)
+        weight = total * scale
+        rest = dot(defect, second)
+        minus_square = dot(-total, total, (1, 1))
+        total_raw = dot(weight, grams[b]) * scale
+        total_gram = (
+            total_raw - dot(dot(total, first, (1, 1)), total) + dot(minus_square, rest)
+        )
+        leading = energy - minus_square
         square = dot(leading, leading) + dot(total_gram, total, (1, 1))
         tail = dot(leading, total)
+        grown = dot(leading, root)
+        if more:
+            mixed = dot(energy, cross) - dot(-weight, rows[b])
+            upcoming = mixed[:, step * b + step : step * b + 2 * step]
+            held = dot(energy, first)
+            mixed_gram = (
+                dot(dot(energy, gram_basis), energy)
+                + dot(held, total, (1, 1))
+                + dot(total, held, (1, 1))
+                + dot(total_raw, total, (1, 1))
+            )
+        if b:
+            of_basis = dot(energy, of_basis)
+            of_raw = jnp.concatenate([dot(energy, of_raw), weight], axis=1)
+        else:
+            of_basis = energy
+            of_raw = weight
         inverse = eliminate(square, True)
-        from_old = dot(inverse, energy)
-        from_new = dot(inverse, total)
-        root = dot(inverse, dot(leading, root))
+        root = dot(inverse, grown)
         tail = dot(inverse, tail) + dot(inverse, total_gram)
+        if more:
+            first = dot(inverse, upcoming) * scales[b + 1]
+            gram_basis = dot(dot(inverse, mixed_gram), inverse, (1, 1))
+            cross = dot(inverse, mixed)
         energy = dot(root, root, (1, 1)) + dot(tail, tail, (1, 1))
-        if b + 1 < BATCHES:
+        if more:
             root = jnp.concatenate([root, tail], axis=1)
-            left = dot(from_old, gram_basis) + dot(from_new, first, (1, 1))
-            right = dot(from_old, first) + dot(from_new, grams[b])
-            gram_basis = dot(left, from_old, (1, 1)) + dot(right, from_new, (1, 1))
-            cross = dot(from_old, cross) + dot(from_new, rows[b])
-        if b == 0:
-            of_basis = from_old
-            of_raw = from_new
-        else:
-            of_basis = dot(from_old, of_basis)
-            of_raw = jnp.concatenate([dot(from_old, of_raw), from_new], axis=1)
+        of_basis = dot(inverse, of_basis)
+        of_raw = dot(inverse, of_raw)
+    raw = jnp.concatenate(by_batch(received_ref[...]), axis=0)
+    parts = dot_short(jnp.concatenate(three_parts(of_raw), axis=0), raw)
+    made_ref[...] = (
+        dot(of_basis, basis_ref[...]) + parts[2 * rank :] + parts[rank : 2 * rank] + parts[:rank]
+    )
+    out = pltpu.make_async_copy(made_ref, new_basis_ref, sent)
+    out.start()
     new_core_ref[...] = eliminate(energy, False)
-    of_raw = of_raw * across
-    raw = jnp.concatenate(by_batch(received), axis=0)
-    parts = dot_short(jnp.concatenate(three_parts(of_raw), axis=0), raw)
-    rank = of_raw.shape[0]
-    new_basis_ref[...] = (
-        dot(of_basis, basis_ref[...]) + parts[2 * rank :] + parts[rank : 2 * rank] + parts[:rank]
-    )
-
-
-def body(basis, core, snapshots):
-    batches, mine, dofs = snapshots.shape
-    grp = lax.axis_size("grp")
+    out.wait()
+
+
+def gram_call(received, basis):
+    groups, batches, mine, dofs = received.shape
+    return pl.pallas_call(
+        gram_kernel,
+        out_shape=jax.ShapeDtypeStruct((3 * groups * mine + basis.shape[0], LANES), jnp.float32),
+        compiler_params=SMALL_GRANT,
+    )(received, basis)
+
+
+def update_call(packed, core, basis, received):
+    groups, batches, mine, dofs = received.shape
     rank = basis.shape[0]
-    cols = grp * mine
-    pieces = snapshots.reshape(batches, mine, grp, dofs // grp).transpose(2, 0, 1, 3)
-    received = exchange(pieces, "grp")
-    packed = pl.pallas_call(
-        gram_kernel, out_shape=jax.ShapeDtypeStruct((3 * cols + rank, LANES), jnp.float32)
-    )(received, basis)
-    packed = total_over_all(packed)
     return pl.pallas_call(
         update_kernel,
         out_shape=(
             jax.ShapeDtypeStruct(basis.shape, jnp.float32),
             jax.ShapeDtypeStruct(core.shape, jnp.float32),
-            jax.ShapeDtypeStruct((batches, rank, cols), jnp.float32),
+            jax.ShapeDtypeStruct((batches, rank, groups * mine), jnp.float32),
         ),
+        out_specs=(
+            pl.BlockSpec(memory_space=pl.ANY),
+            pl.BlockSpec(memory_space=pltpu.VMEM),
+            pl.BlockSpec(memory_space=pltpu.VMEM),
+        ),
+        scratch_shapes=[pltpu.VMEM(basis.shape, jnp.float32), pltpu.SemaphoreType.DMA],
+        compiler_params=SMALL_GRANT,
     )(packed, core, basis, received)
+
+
+def body(basis, core, snapshots):
+    batches, mine, dofs = snapshots.shape
+    grp = lax.axis_size("grp")
+    pieces = snapshots.reshape(batches, mine, grp, dofs // grp).transpose(2, 0, 1, 3)
+    received = exchange(pieces, "grp")
+    packed = total_over_all(gram_call(received, basis))
+    return update_call(packed, core, basis, received)
 
 
 def solution(mesh):

time: 84.2 us -> 79.3 us (0.942)
  Pallas kernels: 15.7 us -> 11.1 us
    pallas_call x2, Pallas kernels: 15.7 us -> 11.1 us  [the longest x1 10.4 us: update_call(): pl.pallas_call(update_kernel, out_shape=(jax.ShapeDtypeStruct(basis.shape...]
where the time goes in v3:
time: 79.3 us; the launch traced here: 78.9 us
  blocking collectives  66 us (83%)
  Pallas kernels  11.1 us (14%)
  local copies, waits for them, and re-layouts  1.11 us (1%)
    all_to_all x4, blocking collectives, exchange(): return lax.all_to_all(parts, axis, split_axis=0, concat_axis=0, tiled=True)  66 us
    pallas_call x1, Pallas kernels, update_call(): pl.pallas_call(update_kernel, out_shape=(jax.ShapeDtypeStruct(basis.shape...  10.4 us

profile of v3, /device:TPU:1, one launch (start us, length us, event | category | flops | bytes accessed | tf_op | source)
XLA Modules:
  0.0 78.9 jit_solution(5543019437717615446)
XLA Ops:
  0.6 1.1 %copy.13 = bf16[4,1,4,8,2048]{4,3,1,0,2:T(8,128)(2,1)S(1)} copy(bf16[4,1,4,8,2048]{4,3,2,1,0:T(8,128)(2,1)} %bitcast.12) | data formatting | bytes 1048576 | tf_op jit(solution)/shard_map/reshape | solution.py:247
  1.7 0.0 copy-start
  1.7 11.7 %all_to_all.20.received_ref = bf16[4,4,8,2048]{3,2,1,0:T(8,128)(2,1)S(1)} all-to-all(bf16[4,4,8,2048]{3,2,1,0:T(8,128)(2,1)S(1)} %bitcast.11), channel_id=1, replica_groups=mesh['rows_0'=4,'rows_1'=16,'rows_2'=2,'grp'=4] {'grp'}, dimensions={0} | all-to-all | bytes 1048576 | tf_op jit(solution)/shard_map/all_to_all | solution.py:22
  13.4 0.0 copy-done
  13.4 0.7 shard_map.58
  14.1 15.8 %all_to_all.21 = f32[32,4,128]{2,1,0:T(4,128)S(1)} all-to-all(f32[32,4,128]{2,1,0:T(4,128)S(1)} %bitcast.10), channel_id=1, replica_groups=mesh['rows_0'=4,'rows_1'=16,'rows_2'=2,'grp'=4] {'rows_0','rows_2','grp'}, dimensions={0} | all-to-all | bytes 131072 | tf_op jit(solution)/shard_map/all_to_all | solution.py:22
  29.9 26.2 %all_to_all.22 = f32[16,4,128]{2,1,0:T(4,128)S(1)} all-to-all(f32[16,4,128]{2,1,0:T(4,128)S(1)} %broadcast_in_dim.6), channel_id=1, replica_groups=mesh['rows_0'=4,'rows_1'=16,'rows_2'=2,'grp'=4] {'rows_1'}, dimensions={0} | all-to-all | bytes 65536 | tf_op jit(solution)/shard_map/all_to_all | solution.py:22
  56.2 0.0 copy-start.1
  56.2 12.4 %all_to_all.23 = f32[32,4,128]{2,1,0:T(4,128)S(1)} all-to-all(f32[32,4,128]{2,1,0:T(4,128)S(1)} %broadcast_in_dim.7), channel_id=1, replica_groups=mesh['rows_0'=4,'rows_1'=16,'rows_2'=2,'grp'=4] {'rows_0','rows_2','grp'}, dimensions={0} | all-to-all | bytes 131072 | tf_op jit(solution)/shard_map/all_to_all | solution.py:22
  68.5 0.0 copy-done.1
  68.6 10.4 %shard_map.59 = (f32[32,2048]{1,0:T(8,128)}, f32[32,32]{1,0:T(8,128)}, f32[4,32,32]{2,1,0:T(8,128)}) custom-call(f32[128,128]{1,0:T(8,128)S(1)} %bitcast.9, f32[32,32]{1,0:T(8,128)S(1)} %copy-done.1, f32[32,2048]{1,0:T(8,128)S(1)} %copy-done, bf16[4,4,8,2048]{3,2,1,0:T(8,128)(2,1)S(1)} %all_to_all.20.received_ref), custom_call_target="tpu_custom_call" | custom-call | tf_op jit(solution)/shard_map/pallas_call | solution.py:227
  (4 shorter events, 0.1 us)
Async XLA Ops:
  1.7 11.7 %copy-start = (f32[32,2048]{1,0:T(8,128)S(1)}, f32[32,2048]{1,0:T(8,128)}, u32[]{:S(2)}) copy-start(f32[32,2048]{1,0:T(8,128)} %basis_ref.3) | copy-start | bytes 786436
  56.2 12.4 %copy-start.1 = (f32[32,32]{1,0:T(8,128)S(1)}, f32[32,32]{1,0:T(8,128)}, u32[]{:S(2)}) copy-start(f32[32,32]{1,0:T(8,128)} %core_ref.1) | copy-start | bytes 12292

commit v4 on v3

--- a/solution.py
+++ b/solution.py
@@ -13,6 +13,7 @@
 FAR = "rows_1"
 LANES = 128
 SUB = 8
+CHUNKS = 1
 SMALL_GRANT = pltpu.CompilerParams(vmem_limit_bytes=8 * 2**20)
 
 epsilon = 1e-06
@@ -65,10 +66,12 @@
     ]
 
 
-def gram_kernel(received_ref, basis_ref, packed_ref):
+def gram_kernel(received_ref, basis_ref, packed_ref, held_ref):
     raw = jnp.concatenate(by_batch(received_ref[...]), axis=0)
     parts = jnp.concatenate(three_parts(basis_ref[...]), axis=0)
     cols = raw.shape[0]
+    held_ref[:cols] = raw
+    held_ref[cols:] = parts
     rank = basis_ref.shape[0]
     raw_gram = dot_short(raw, raw, (1, 1))
     cross = dot_short(parts, raw, (1, 1))
@@ -90,54 +93,49 @@
 def eliminate(matrix, want_inverse):
     order = matrix.shape[0]
     tiles = order // SUB
-    work = [matrix[SUB * g : SUB * g + SUB] for g in range(tiles)]
     row = lax.broadcasted_iota(jnp.int32, (SUB, order), 0)
     lane = lax.broadcasted_iota(jnp.int32, (SUB, order), 1)
     inverse = [jnp.where(row + SUB * g == lane, 1.0, 0.0) for g in range(tiles)]
     lower = [jnp.zeros((SUB, order), jnp.float32) for g in range(tiles)]
+    scale = [jnp.zeros((SUB, order), jnp.float32) for g in range(tiles)]
 
     def spread(tile, k):
         return jnp.broadcast_to(tile[k : k + 1], (SUB, order))
 
-    for p in range(tiles):
-        columns = {
-            (m, g): jnp.broadcast_to(work[g][:, SUB * p + m : SUB * p + m + 1], (SUB, order))
-            for m in range(SUB)
-            for g in range(p, tiles)
-        }
-        scale = jnp.zeros((SUB, order), jnp.float32)
-        for k in range(SUB):
-            pivot = spread(columns[k, p], k)
-            root = lax.rsqrt(pivot)
-            recip = 1.0 / pivot
-            scale = jnp.where(row == k, root, scale)
-            factors = {g: columns[k, g] * recip for g in range(p, tiles)}
-            factors[p] = jnp.where(row > k, factors[p], 0.0)
-            if not want_inverse:
-                for g in range(p, tiles):
-                    part = columns[k, g] * root
-                    if g == p:
-                        part = jnp.where(row >= k, part, 0.0)
-                    lower[g] = jnp.where(lane == SUB * p + k, part, lower[g])
-            for m in range(k + 1, SUB):
-                top = spread(columns[m, p], k)
-                for g in range(p, tiles):
-                    columns[m, g] = columns[m, g] - factors[g] * top
-            top = spread(work[p], k)
-            for g in range(p + 1, tiles):
-                work[g] = work[g] - factors[g] * top
-            work[p] = work[p] - factors[p] * top
-            if want_inverse:
-                top = spread(inverse[p], k)
-                for g in range(p, tiles):
-                    inverse[g] = inverse[g] - factors[g] * top
+    columns = {
+        (m, g): jnp.broadcast_to(matrix[SUB * g : SUB * g + SUB, m : m + 1], (SUB, order))
+        for m in range(order)
+        for g in range(m // SUB, tiles)
+    }
+    for j in range(order):
+        p, k = divmod(j, SUB)
+        pivot = spread(columns[j, p], k)
+        root = lax.rsqrt(pivot)
+        recip = 1.0 / pivot
+        scale[p] = jnp.where(row == k, root, scale[p])
+        factors = {g: columns[j, g] * recip for g in range(p, tiles)}
+        factors[p] = jnp.where(row > k, factors[p], 0.0)
+        if not want_inverse:
+            for g in range(p, tiles):
+                part = columns[j, g] * root
+                if g == p:
+                    part = jnp.where(row >= k, part, 0.0)
+                lower[g] = jnp.where(lane == j, part, lower[g])
+        for m in range(j + 1, order):
+            top = spread(columns[j, m // SUB], m % SUB)
+            for g in range(m // SUB, tiles):
+                columns[m, g] = columns[m, g] - factors[g] * top
         if want_inverse:
-            inverse[p] = inverse[p] * scale
-    return jnp.concatenate(inverse if want_inverse else lower, axis=0)
+            top = spread(inverse[p], k)
+            for g in range(p, tiles):
+                inverse[g] = inverse[g] - factors[g] * top
+    if want_inverse:
+        return jnp.concatenate([inverse[g] * scale[g] for g in range(tiles)], axis=0)
+    return jnp.concatenate(lower, axis=0)
 
 
 def update_kernel(
-    packed_ref, core_ref, basis_ref, received_ref, new_basis_ref, new_core_ref, firsts_ref, made_ref, sent
+    packed_ref, core_ref, held_ref, new_basis_ref, new_core_ref, firsts_ref, made_ref, sent
 ):
     cols = packed_ref.shape[1]
     step = cols // BATCHES
@@ -185,6 +183,8 @@
             )
         if b:
             of_basis = dot(energy, of_basis)
+            if not more:
+                of_basis = jnp.concatenate([of_basis] * 3, axis=1)
             of_raw = jnp.concatenate([dot(energy, of_raw), weight], axis=1)
         else:
             of_basis = energy
@@ -201,53 +201,72 @@
             root = jnp.concatenate([root, tail], axis=1)
         of_basis = dot(inverse, of_basis)
         of_raw = dot(inverse, of_raw)
-    raw = jnp.concatenate(by_batch(received_ref[...]), axis=0)
-    parts = dot_short(jnp.concatenate(three_parts(of_raw), axis=0), raw)
-    made_ref[...] = (
-        dot(of_basis, basis_ref[...]) + parts[2 * rank :] + parts[rank : 2 * rank] + parts[:rank]
-    )
-    out = pltpu.make_async_copy(made_ref, new_basis_ref, sent)
-    out.start()
+    basis_parts = three_parts(of_basis)
+    part = lax.broadcasted_iota(jnp.int32, of_basis.shape, 1) // rank
+    basis_parts = [
+        jnp.where(part < 3 - n, basis_parts[n].astype(jnp.float32), 0.0).astype(jnp.bfloat16) for n in range(3)
+    ]
+    mixing = jnp.concatenate(
+        [jnp.concatenate(three_parts(of_raw), axis=0), jnp.concatenate(basis_parts, axis=0)], axis=1
+    )
+    chunk = made_ref.shape[2]
+    copies = []
+    for n in range(CHUNKS):
+        made = dot_short(mixing, held_ref[:, chunk * n : chunk * n + chunk])
+        made_ref[n] = made[2 * rank :] + made[rank : 2 * rank] + made[:rank]
+        copies.append(
+            pltpu.make_async_copy(
+                made_ref.at[n], new_basis_ref.at[:, pl.ds(chunk * n, chunk)], sent.at[n]
+            )
+        )
+        copies[n].start()
     new_core_ref[...] = eliminate(energy, False)
-    out.wait()
+    for out in copies:
+        out.wait()
 
 
 def gram_call(received, basis):
     groups, batches, mine, dofs = received.shape
     return pl.pallas_call(
         gram_kernel,
-        out_shape=jax.ShapeDtypeStruct((3 * groups * mine + basis.shape[0], LANES), jnp.float32),
+        out_shape=(
+            jax.ShapeDtypeStruct((3 * groups * mine + basis.shape[0], LANES), jnp.float32),
+            jax.ShapeDtypeStruct((batches * groups * mine + 3 * basis.shape[0], dofs), jnp.bfloat16),
+        ),
         compiler_params=SMALL_GRANT,
     )(received, basis)
 
 
-def update_call(packed, core, basis, received):
-    groups, batches, mine, dofs = received.shape
-    rank = basis.shape[0]
+def update_call(packed, core, held):
+    rank = core.shape[0]
+    dofs = held.shape[1]
+    step = packed.shape[1] // BATCHES
     return pl.pallas_call(
         update_kernel,
         out_shape=(
-            jax.ShapeDtypeStruct(basis.shape, jnp.float32),
-            jax.ShapeDtypeStruct(core.shape, jnp.float32),
-            jax.ShapeDtypeStruct((batches, rank, groups * mine), jnp.float32),
+            jax.ShapeDtypeStruct((rank, dofs), jnp.float32),
+            jax.ShapeDtypeStruct((rank, rank), jnp.float32),
+            jax.ShapeDtypeStruct((BATCHES, rank, step), jnp.float32),
         ),
         out_specs=(
             pl.BlockSpec(memory_space=pl.ANY),
             pl.BlockSpec(memory_space=pltpu.VMEM),
             pl.BlockSpec(memory_space=pltpu.VMEM),
         ),
-        scratch_shapes=[pltpu.VMEM(basis.shape, jnp.float32), pltpu.SemaphoreType.DMA],
+        scratch_shapes=[
+            pltpu.VMEM((CHUNKS, rank, dofs // CHUNKS), jnp.float32),
+            pltpu.SemaphoreType.DMA((CHUNKS,)),
+        ],
         compiler_params=SMALL_GRANT,
-    )(packed, core, basis, received)
+    )(packed, core, held)
 
 
 def body(basis, core, snapshots):
     batches, mine, dofs = snapshots.shape
     grp = lax.axis_size("grp")
     pieces = snapshots.reshape(batches, mine, grp, dofs // grp).transpose(2, 0, 1, 3)
-    received = exchange(pieces, "grp")
-    packed = total_over_all(gram_call(received, basis))
-    return update_call(packed, core, basis, received)
+    packed, held = gram_call(exchange(pieces, "grp"), basis)
+    return update_call(total_over_all(packed), core, held)
 
 
 def solution(mesh):

time: 79.3 us -> 78.1 us (0.985)
  Pallas kernels: 11.1 us -> 9.85 us
    pallas_call x2, Pallas kernels: 11.1 us -> 9.85 us  [the longest x1 9.17 us: update_call(): pl.pallas_call(update_kernel, out_shape=(jax.ShapeDtypeStruct((rank, dofs...]
where the time goes in v4:
time: 78.1 us; the launch traced here: 77.7 us
  blocking collectives  66 us (85%)
  Pallas kernels  9.85 us (13%)
  local copies, waits for them, and re-layouts  1.11 us (1%)
    all_to_all x4, blocking collectives, exchange(): return lax.all_to_all(parts, axis, split_axis=0, concat_axis=0, tiled=True)  66 us
    pallas_call x1, Pallas kernels, update_call(): pl.pallas_call(update_kernel, out_shape=(jax.ShapeDtypeStruct((rank, dofs...  9.17 us

profile of v4, /device:TPU:1, one launch (start us, length us, event | category | flops | bytes accessed | tf_op | source)
XLA Modules:
  0.0 77.7 jit_solution(4094803082644930764)
XLA Ops:
  0.6 1.1 %copy.13 = bf16[4,1,4,8,2048]{4,3,1,0,2:T(8,128)(2,1)S(1)} copy(bf16[4,1,4,8,2048]{4,3,2,1,0:T(8,128)(2,1)} %bitcast.12) | data formatting | bytes 1048576 | tf_op jit(solution)/shard_map/reshape | solution.py:267
  1.7 0.0 copy-start
  1.7 11.7 %all_to_all.20.received_ref = bf16[4,4,8,2048]{3,2,1,0:T(8,128)(2,1)S(1)} all-to-all(bf16[4,4,8,2048]{3,2,1,0:T(8,128)(2,1)S(1)} %bitcast.11), channel_id=1, replica_groups=mesh['rows_0'=4,'rows_1'=16,'rows_2'=2,'grp'=4] {'grp'}, dimensions={0} | all-to-all | bytes 1048576 | tf_op jit(solution)/shard_map/all_to_all | solution.py:23
  13.4 0.0 copy-done
  13.4 0.7 shard_map.58
  14.1 15.8 %all_to_all.21 = f32[32,4,128]{2,1,0:T(4,128)S(1)} all-to-all(f32[32,4,128]{2,1,0:T(4,128)S(1)} %bitcast.10), channel_id=1, replica_groups=mesh['rows_0'=4,'rows_1'=16,'rows_2'=2,'grp'=4] {'rows_0','rows_2','grp'}, dimensions={0} | all-to-all | bytes 131072 | tf_op jit(solution)/shard_map/all_to_all | solution.py:23
  29.9 26.2 %all_to_all.22 = f32[16,4,128]{2,1,0:T(4,128)S(1)} all-to-all(f32[16,4,128]{2,1,0:T(4,128)S(1)} %broadcast_in_dim.6), channel_id=1, replica_groups=mesh['rows_0'=4,'rows_1'=16,'rows_2'=2,'grp'=4] {'rows_1'}, dimensions={0} | all-to-all | bytes 65536 | tf_op jit(solution)/shard_map/all_to_all | solution.py:23
  56.2 0.0 copy-start.1
  56.2 12.4 %all_to_all.23 = f32[32,4,128]{2,1,0:T(4,128)S(1)} all-to-all(f32[32,4,128]{2,1,0:T(4,128)S(1)} %broadcast_in_dim.7), channel_id=1, replica_groups=mesh['rows_0'=4,'rows_1'=16,'rows_2'=2,'grp'=4] {'rows_0','rows_2','grp'}, dimensions={0} | all-to-all | bytes 131072 | tf_op jit(solution)/shard_map/all_to_all | solution.py:23
  68.6 0.0 copy-done.1
  68.6 9.2 %shard_map.59 = (f32[32,2048]{1,0:T(8,128)}, f32[32,32]{1,0:T(8,128)}, f32[4,32,32]{2,1,0:T(8,128)}) custom-call(f32[128,128]{1,0:T(8,128)S(1)} %bitcast.9, f32[32,32]{1,0:T(8,128)S(1)} %copy-done.1, bf16[224,2048]{1,0:T(8,128)(2,1)S(1)} %get-tuple-element.6.held_ref), custom_call_target="tpu_custom_call" | custom-call | tf_op jit(solution)/shard_map/pallas_call | solution.py:244
  (4 shorter events, 0.1 us)
Async XLA Ops:
  1.7 11.7 %copy-start = (f32[32,2048]{1,0:T(8,128)S(1)}, f32[32,2048]{1,0:T(8,128)}, u32[]{:S(2)}) copy-start(f32[32,2048]{1,0:T(8,128)} %basis_ref.1) | copy-start | bytes 786436
  56.2 12.4 %copy-start.1 = (f32[32,32]{1,0:T(8,128)S(1)}, f32[32,32]{1,0:T(8,128)}, u32[]{:S(2)}) copy-start(f32[32,32]{1,0:T(8,128)} %core_ref.1) | copy-start | bytes 12292

commit v5 on v4

--- a/solution.py
+++ b/solution.py
@@ -13,7 +13,7 @@
 FAR = "rows_1"
 LANES = 128
 SUB = 8
-CHUNKS = 1
+CHUNKS = 2
 SMALL_GRANT = pltpu.CompilerParams(vmem_limit_bytes=8 * 2**20)
 
 epsilon = 1e-06
@@ -33,13 +33,14 @@
 
 
 def dot(left, right, contract=(1, 0)):
-    return lax.dot_general(
-        left,
-        right,
-        (((contract[0],), (contract[1],)), ((), ())),
-        precision=lax.Precision.HIGHEST,
-        preferred_element_type=jnp.float32,
-    )
+    rows = left.shape[0]
+    lefts = three_parts(left)
+    high, middle, low = three_parts(right)
+    first = dot_short(jnp.concatenate(lefts, axis=0), high, contract)
+    second = dot_short(jnp.concatenate(lefts[:2], axis=0), middle, contract)
+    third = dot_short(lefts[0], low, contract)
+    small = first[2 * rows :] + second[rows:] + third
+    return first[:rows] + ((first[rows : 2 * rows] + second[:rows]) + small)
 
 
 def dot_short(left, right, contract=(1, 0)):
@@ -49,6 +50,14 @@
         (((contract[0],), (contract[1],)), ((), ())),
         preferred_element_type=jnp.float32,
     )
+
+
+def dot_middle(left, right):
+    rows = left.shape[0]
+    high, middle, low = three_parts(left)
+    right_high, right_middle, right_low = three_parts(right)
+    first = dot_short(jnp.concatenate([high, middle], axis=0), right_high)
+    return first[:rows] + (first[rows:] + dot_short(high, right_middle))
 
 
 def three_parts(values):
@@ -90,17 +99,19 @@
     packed_ref[3 * step :] = cross
 
 
-def eliminate(matrix, want_inverse):
+def eliminate(matrix, rights=(), want_inverse=True):
     order = matrix.shape[0]
     tiles = order // SUB
     row = lax.broadcasted_iota(jnp.int32, (SUB, order), 0)
     lane = lax.broadcasted_iota(jnp.int32, (SUB, order), 1)
-    inverse = [jnp.where(row + SUB * g == lane, 1.0, 0.0) for g in range(tiles)]
+    solved = [[r[SUB * g : SUB * g + SUB] for g in range(tiles)] for r in rights]
+    if want_inverse:
+        solved.insert(0, [jnp.where(row + SUB * g == lane, 1.0, 0.0) for g in range(tiles)])
     lower = [jnp.zeros((SUB, order), jnp.float32) for g in range(tiles)]
     scale = [jnp.zeros((SUB, order), jnp.float32) for g in range(tiles)]
 
     def spread(tile, k):
-        return jnp.broadcast_to(tile[k : k + 1], (SUB, order))
+        return jnp.broadcast_to(tile[k : k + 1], tile.shape)
 
     columns = {
         (m, g): jnp.broadcast_to(matrix[SUB * g : SUB * g + SUB, m : m + 1], (SUB, order))
@@ -125,13 +136,13 @@
             top = spread(columns[j, m // SUB], m % SUB)
             for g in range(m // SUB, tiles):
                 columns[m, g] = columns[m, g] - factors[g] * top
-        if want_inverse:
-            top = spread(inverse[p], k)
+        for right in solved:
+            top = spread(right[p], k)
             for g in range(p, tiles):
-                inverse[g] = inverse[g] - factors[g] * top
-    if want_inverse:
-        return jnp.concatenate([inverse[g] * scale[g] for g in range(tiles)], axis=0)
-    return jnp.concatenate(lower, axis=0)
+                right[g] = right[g] - factors[g] * top
+    if not want_inverse:
+        return jnp.concatenate(lower, axis=0)
+    return [jnp.concatenate([right[g] * scale[g] for g in range(tiles)], axis=0) for right in solved]
 
 
 def update_kernel(
@@ -158,14 +169,14 @@
         scale = scales[b]
         firsts_ref[b] = first
         defect = eye - gram_basis
-        second = dot(defect, first)
+        second = dot_middle(defect, first)
         total = first + second
         weight = total * scale
-        rest = dot(defect, second)
+        rest = dot_middle(defect, second)
         minus_square = dot(-total, total, (1, 1))
         total_raw = dot(weight, grams[b]) * scale
         total_gram = (
-            total_raw - dot(dot(total, first, (1, 1)), total) + dot(minus_square, rest)
+            total_raw - dot(dot(total, first, (1, 1)), total) + dot_middle(minus_square, rest)
         )
         leading = energy - minus_square
         square = dot(leading, leading) + dot(total_gram, total, (1, 1))
@@ -189,7 +200,7 @@
         else:
             of_basis = energy
             of_raw = weight
-        inverse = eliminate(square, True)
+        (inverse,) = eliminate(square)
         root = dot(inverse, grown)
         tail = dot(inverse, tail) + dot(inverse, total_gram)
         if more:
@@ -220,7 +231,7 @@
             )
         )
         copies[n].start()
-    new_core_ref[...] = eliminate(energy, False)
+    new_core_ref[...] = eliminate(energy, want_inverse=False)
     for out in copies:
         out.wait()
 

time: 78.1 us -> 76.7 us (0.982)
  Pallas kernels: 9.85 us -> 8.53 us
    pallas_call x1, Pallas kernels: 9.17 us -> 7.85 us  [update_call(): pl.pallas_call(update_kernel, out_shape=(jax.ShapeDtypeStruct((rank, dofs...]
where the time goes in v5:
time: 76.7 us; the launch traced here: 76.4 us
  blocking collectives  66 us (86%)
  Pallas kernels  8.53 us (11%)
  local copies, waits for them, and re-layouts  1.11 us (1%)
    all_to_all x4, blocking collectives, exchange(): return lax.all_to_all(parts, axis, split_axis=0, concat_axis=0, tiled=True)  66 us
    pallas_call x1, Pallas kernels, update_call(): pl.pallas_call(update_kernel, out_shape=(jax.ShapeDtypeStruct((rank, dofs...  7.85 us

profile of v5, /device:TPU:1, one launch (start us, length us, event | category | flops | bytes accessed | tf_op | source)
XLA Modules:
  0.0 76.4 jit_solution(2744430681965583946)
XLA Ops:
  0.6 1.1 %copy.13 = bf16[4,1,4,8,2048]{4,3,1,0,2:T(8,128)(2,1)S(1)} copy(bf16[4,1,4,8,2048]{4,3,2,1,0:T(8,128)(2,1)} %bitcast.12) | data formatting | bytes 1048576 | tf_op jit(solution)/shard_map/reshape | solution.py:278
  1.7 0.0 copy-start
  1.7 11.7 %all_to_all.20.received_ref = bf16[4,4,8,2048]{3,2,1,0:T(8,128)(2,1)S(1)} all-to-all(bf16[4,4,8,2048]{3,2,1,0:T(8,128)(2,1)S(1)} %bitcast.11), channel_id=1, replica_groups=mesh['rows_0'=4,'rows_1'=16,'rows_2'=2,'grp'=4] {'grp'}, dimensions={0} | all-to-all | bytes 1048576 | tf_op jit(solution)/shard_map/all_to_all | solution.py:23
  13.4 0.0 copy-done
  13.4 0.7 shard_map.58
  14.1 15.8 %all_to_all.21 = f32[32,4,128]{2,1,0:T(4,128)S(1)} all-to-all(f32[32,4,128]{2,1,0:T(4,128)S(1)} %bitcast.10), channel_id=1, replica_groups=mesh['rows_0'=4,'rows_1'=16,'rows_2'=2,'grp'=4] {'rows_0','rows_2','grp'}, dimensions={0} | all-to-all | bytes 131072 | tf_op jit(solution)/shard_map/all_to_all | solution.py:23
  29.9 26.2 %all_to_all.22 = f32[16,4,128]{2,1,0:T(4,128)S(1)} all-to-all(f32[16,4,128]{2,1,0:T(4,128)S(1)} %broadcast_in_dim.6), channel_id=1, replica_groups=mesh['rows_0'=4,'rows_1'=16,'rows_2'=2,'grp'=4] {'rows_1'}, dimensions={0} | all-to-all | bytes 65536 | tf_op jit(solution)/shard_map/all_to_all | solution.py:23
  56.2 0.0 copy-start.1
  56.2 12.4 %all_to_all.23 = f32[32,4,128]{2,1,0:T(4,128)S(1)} all-to-all(f32[32,4,128]{2,1,0:T(4,128)S(1)} %broadcast_in_dim.7), channel_id=1, replica_groups=mesh['rows_0'=4,'rows_1'=16,'rows_2'=2,'grp'=4] {'rows_0','rows_2','grp'}, dimensions={0} | all-to-all | bytes 131072 | tf_op jit(solution)/shard_map/all_to_all | solution.py:23
  68.6 0.0 copy-done.1
  68.6 7.9 %shard_map.59 = (f32[32,2048]{1,0:T(8,128)}, f32[32,32]{1,0:T(8,128)}, f32[4,32,32]{2,1,0:T(8,128)}) custom-call(f32[128,128]{1,0:T(8,128)S(1)} %bitcast.9, f32[32,32]{1,0:T(8,128)S(1)} %copy-done.1, bf16[224,2048]{1,0:T(8,128)(2,1)S(1)} %get-tuple-element.6.held_ref), custom_call_target="tpu_custom_call" | custom-call | tf_op jit(solution)/shard_map/pallas_call | solution.py:255
  (4 shorter events, 0.1 us)
Async XLA Ops:
  1.7 11.7 %copy-start = (f32[32,2048]{1,0:T(8,128)S(1)}, f32[32,2048]{1,0:T(8,128)}, u32[]{:S(2)}) copy-start(f32[32,2048]{1,0:T(8,128)} %basis_ref.1) | copy-start | bytes 786436
  56.2 12.4 %copy-start.1 = (f32[32,32]{1,0:T(8,128)S(1)}, f32[32,32]{1,0:T(8,128)}, u32[]{:S(2)}) copy-start(f32[32,32]{1,0:T(8,128)} %core_ref.1) | copy-start | bytes 12292

commit v6 on v5

--- a/solution.py
+++ b/solution.py
@@ -9,7 +9,8 @@
 BATCHES = 4
 ROWS_GRP = ("rows_0", "rows_1", "rows_2", "grp")
 ROWS = ("rows_0", "rows_1", "rows_2")
-NEAR = ("rows_0", "rows_2", "grp")
+NEAR = ("rows_0", "grp")
+CORE = "rows_2"
 FAR = "rows_1"
 LANES = 128
 SUB = 8
@@ -25,11 +26,13 @@
 
 def total_over_all(packed):
     near = lax.axis_size(NEAR)
+    cores = lax.axis_size(CORE)
     far = lax.axis_size(FAR)
     rows, lanes = packed.shape
-    piece = exchange(packed.reshape(near, rows // near, lanes), NEAR).sum(axis=0)
-    piece = exchange(jnp.broadcast_to(piece, (far, *piece.shape)), FAR).sum(axis=0)
-    return exchange(jnp.broadcast_to(piece, (near, *piece.shape)), NEAR).reshape(rows, lanes)
+    piece = exchange(packed.reshape(near * cores, rows // (near * cores), lanes), (*NEAR, CORE)).sum(axis=0)
+    pieces = exchange(jnp.broadcast_to(piece, (far * cores, *piece.shape)), (FAR, CORE))
+    pair = pieces.reshape(far, cores, *piece.shape).sum(axis=0).reshape(rows // near, lanes)
+    return exchange(jnp.broadcast_to(pair, (near, *pair.shape)), NEAR).reshape(rows, lanes)
 
 
 def dot(left, right, contract=(1, 0)):

time: 76.7 us -> 76.6 us (level)
  no operation moved by 1% of the time
where the time goes in v6:
time: 76.6 us; the launch traced here: 75.7 us
  blocking collectives  65.4 us (85%)
  Pallas kernels  8.53 us (11%)
  local copies, waits for them, and re-layouts  1.11 us (1%)
    all_to_all x4, blocking collectives, exchange(): return lax.all_to_all(parts, axis, split_axis=0, concat_axis=0, tiled=True)  65.4 us
    pallas_call x1, Pallas kernels, update_call(): pl.pallas_call(update_kernel, out_shape=(jax.ShapeDtypeStruct((rank, dofs...  7.85 us

profile of v6, /device:TPU:1, one launch (start us, length us, event | category | flops | bytes accessed | tf_op | source)
XLA Modules:
  0.0 75.7 jit_solution(14975330553154556443)
XLA Ops:
  0.6 1.1 %copy.18 = bf16[4,1,4,8,2048]{4,3,1,0,2:T(8,128)(2,1)S(1)} copy(bf16[4,1,4,8,2048]{4,3,2,1,0:T(8,128)(2,1)} %bitcast.14) | data formatting | bytes 1048576 | tf_op jit(solution)/shard_map/reshape | solution.py:281
  1.7 0.0 copy-start
  1.7 11.7 %all_to_all.20.received_ref = bf16[4,4,8,2048]{3,2,1,0:T(8,128)(2,1)S(1)} all-to-all(bf16[4,4,8,2048]{3,2,1,0:T(8,128)(2,1)S(1)} %bitcast.13), channel_id=1, replica_groups=mesh['rows_0'=4,'rows_1'=16,'rows_2'=2,'grp'=4] {'grp'}, dimensions={0} | all-to-all | bytes 1048576 | tf_op jit(solution)/shard_map/all_to_all | solution.py:24
  13.4 0.0 copy-done
  13.4 0.7 shard_map.58
  14.1 15.8 %all_to_all.21 = f32[32,4,128]{2,1,0:T(4,128)S(1)} all-to-all(f32[32,4,128]{2,1,0:T(4,128)S(1)} %bitcast.12), channel_id=1, replica_groups=mesh['rows_0'=4,'rows_1'=16,'rows_2'=2,'grp'=4] {'rows_0','grp','rows_2'}, dimensions={0} | all-to-all | bytes 131072 | tf_op jit(solution)/shard_map/all_to_all | solution.py:24
  30.0 28.5 %all_to_all.22 = f32[32,4,128]{2,1,0:T(4,128)S(1)} all-to-all(f32[32,4,128]{2,1,0:T(4,128)S(1)} %broadcast_in_dim.6), channel_id=1, replica_groups=mesh['rows_0'=4,'rows_1'=16,'rows_2'=2,'grp'=4] {'rows_1','rows_2'}, dimensions={0} | all-to-all | bytes 131072 | tf_op jit(solution)/shard_map/all_to_all | solution.py:24
  58.5 0.0 copy-start.1
  58.5 9.4 %all_to_all.23 = f32[16,8,128]{2,1,0:T(8,128)S(1)} all-to-all(f32[16,8,128]{2,1,0:T(8,128)S(1)} %broadcast_in_dim.7), channel_id=1, replica_groups=mesh['rows_0'=4,'rows_1'=16,'rows_2'=2,'grp'=4] {'rows_0','grp'}, dimensions={0} | all-to-all | bytes 131072 | tf_op jit(solution)/shard_map/all_to_all | solution.py:24
  67.9 0.0 copy-done.1
  67.9 7.9 %shard_map.59 = (f32[32,2048]{1,0:T(8,128)}, f32[32,32]{1,0:T(8,128)}, f32[4,32,32]{2,1,0:T(8,128)}) custom-call(f32[128,128]{1,0:T(8,128)S(1)} %bitcast.11, f32[32,32]{1,0:T(8,128)S(1)} %copy-done.1, bf16[224,2048]{1,0:T(8,128)(2,1)S(1)} %get-tuple-element.6.held_ref), custom_call_target="tpu_custom_call" | custom-call | tf_op jit(solution)/shard_map/pallas_call | solution.py:258
  (4 shorter events, 0.1 us)
Async XLA Ops:
  1.7 11.7 %copy-start = (f32[32,2048]{1,0:T(8,128)S(1)}, f32[32,2048]{1,0:T(8,128)}, u32[]{:S(2)}) copy-start(f32[32,2048]{1,0:T(8,128)} %basis_ref.1) | copy-start | bytes 786436
  58.5 9.4 %copy-start.1 = (f32[32,32]{1,0:T(8,128)S(1)}, f32[32,32]{1,0:T(8,128)}, u32[]{:S(2)}) copy-start(f32[32,32]{1,0:T(8,128)} %core_ref.1) | copy-start | bytes 12292

commit v7 on v5

--- a/solution.py
+++ b/solution.py
@@ -113,13 +113,25 @@
     def spread(tile, k):
         return jnp.broadcast_to(tile[k : k + 1], tile.shape)
 
-    columns = {
-        (m, g): jnp.broadcast_to(matrix[SUB * g : SUB * g + SUB, m : m + 1], (SUB, order))
-        for m in range(order)
-        for g in range(m // SUB, tiles)
-    }
+    half = order // 2
+    ahead = half // SUB
+    work = [matrix[SUB * g : SUB * g + SUB] for g in range(tiles)]
+    columns = {}
+
+    def take(m, g):
+        columns[m, g] = jnp.broadcast_to(work[g][:, m : m + 1], (SUB, order))
+
+    for m in range(half):
+        for g in range(m // SUB, tiles):
+            take(m, g)
+    for m in range(half, half + SUB):
+        take(m, ahead)
     for j in range(order):
         p, k = divmod(j, SUB)
+        if j == half:
+            for m in range(half, order):
+                for g in range(ahead + 1, tiles):
+                    take(m, g)
         pivot = spread(columns[j, p], k)
         root = lax.rsqrt(pivot)
         recip = 1.0 / pivot
@@ -132,10 +144,14 @@
                 if g == p:
                     part = jnp.where(row >= k, part, 0.0)
                 lower[g] = jnp.where(lane == j, part, lower[g])
-        for m in range(j + 1, order):
+        for m in range(j + 1, half + SUB if j < half else order):
             top = spread(columns[j, m // SUB], m % SUB)
-            for g in range(m // SUB, tiles):
+            for g in range(m // SUB, tiles if m < half or j >= half else ahead + 1):
                 columns[m, g] = columns[m, g] - factors[g] * top
+        if j < half:
+            top = spread(work[p], k)
+            for g in range(p, tiles):
+                work[g] = work[g] - factors[g] * top
         for right in solved:
             top = spread(right[p], k)
             for g in range(p, tiles):

time: 76.7 us -> 76.6 us (level)
  no operation moved by 1% of the time
where the time goes in v7:
time: 76.6 us; the launch traced here: 76.3 us
  blocking collectives  66 us (86%)
  Pallas kernels  8.42 us (11%)
  local copies, waits for them, and re-layouts  1.11 us (1%)
    all_to_all x4, blocking collectives, exchange(): return lax.all_to_all(parts, axis, split_axis=0, concat_axis=0, tiled=True)  66 us
    pallas_call x1, Pallas kernels, update_call(): pl.pallas_call(update_kernel, out_shape=(jax.ShapeDtypeStruct((rank, dofs...  7.74 us

profile of v7, /device:TPU:1, one launch (start us, length us, event | category | flops | bytes accessed | tf_op | source)
XLA Modules:
  0.0 76.3 jit_solution(10925756918816251340)
XLA Ops:
  0.6 1.1 %copy.13 = bf16[4,1,4,8,2048]{4,3,1,0,2:T(8,128)(2,1)S(1)} copy(bf16[4,1,4,8,2048]{4,3,2,1,0:T(8,128)(2,1)} %bitcast.12) | data formatting | bytes 1048576 | tf_op jit(solution)/shard_map/reshape | solution.py:294
  1.7 0.0 copy-start
  1.7 11.7 %all_to_all.20.received_ref = bf16[4,4,8,2048]{3,2,1,0:T(8,128)(2,1)S(1)} all-to-all(bf16[4,4,8,2048]{3,2,1,0:T(8,128)(2,1)S(1)} %bitcast.11), channel_id=1, replica_groups=mesh['rows_0'=4,'rows_1'=16,'rows_2'=2,'grp'=4] {'grp'}, dimensions={0} | all-to-all | bytes 1048576 | tf_op jit(solution)/shard_map/all_to_all | solution.py:23
  13.4 0.0 copy-done
  13.4 0.7 shard_map.58
  14.1 15.8 %all_to_all.21 = f32[32,4,128]{2,1,0:T(4,128)S(1)} all-to-all(f32[32,4,128]{2,1,0:T(4,128)S(1)} %bitcast.10), channel_id=1, replica_groups=mesh['rows_0'=4,'rows_1'=16,'rows_2'=2,'grp'=4] {'rows_0','rows_2','grp'}, dimensions={0} | all-to-all | bytes 131072 | tf_op jit(solution)/shard_map/all_to_all | solution.py:23
  29.9 26.2 %all_to_all.22 = f32[16,4,128]{2,1,0:T(4,128)S(1)} all-to-all(f32[16,4,128]{2,1,0:T(4,128)S(1)} %broadcast_in_dim.6), channel_id=1, replica_groups=mesh['rows_0'=4,'rows_1'=16,'rows_2'=2,'grp'=4] {'rows_1'}, dimensions={0} | all-to-all | bytes 65536 | tf_op jit(solution)/shard_map/all_to_all | solution.py:23
  56.2 0.0 copy-start.1
  56.2 12.4 %all_to_all.23 = f32[32,4,128]{2,1,0:T(4,128)S(1)} all-to-all(f32[32,4,128]{2,1,0:T(4,128)S(1)} %broadcast_in_dim.7), channel_id=1, replica_groups=mesh['rows_0'=4,'rows_1'=16,'rows_2'=2,'grp'=4] {'rows_0','rows_2','grp'}, dimensions={0} | all-to-all | bytes 131072 | tf_op jit(solution)/shard_map/all_to_all | solution.py:23
  68.6 0.0 copy-done.1
  68.6 7.7 %shard_map.59 = (f32[32,2048]{1,0:T(8,128)}, f32[32,32]{1,0:T(8,128)}, f32[4,32,32]{2,1,0:T(8,128)}) custom-call(f32[128,128]{1,0:T(8,128)S(1)} %bitcast.9, f32[32,32]{1,0:T(8,128)S(1)} %copy-done.1, bf16[224,2048]{1,0:T(8,128)(2,1)S(1)} %get-tuple-element.6.held_ref), custom_call_target="tpu_custom_call" | custom-call | tf_op jit(solution)/shard_map/pallas_call | solution.py:271
  (4 shorter events, 0.1 us)
Async XLA Ops:
  1.7 11.7 %copy-start = (f32[32,2048]{1,0:T(8,128)S(1)}, f32[32,2048]{1,0:T(8,128)}, u32[]{:S(2)}) copy-start(f32[32,2048]{1,0:T(8,128)} %basis_ref.1) | copy-start | bytes 786436
  56.2 12.4 %copy-start.1 = (f32[32,32]{1,0:T(8,128)S(1)}, f32[32,32]{1,0:T(8,128)}, u32[]{:S(2)}) copy-start(f32[32,32]{1,0:T(8,128)} %core_ref.1) | copy-start | bytes 12292
